TPU v7x, 32 devices: a whole 2x2x4 slice. The times are simulated.
32 devices in a mesh: dp: 8 (over y, x, core), mp: 4 (over z).
Axes of the slice: x: 2, y: 2, z: 4, core: 2. Of those that a mesh axis runs over, the one named last changes fastest.
Arguments:
- tokens: bfloat16 [4096, 1024], P('dp', 'mp'), may hold values from -150 to 150
- pre_gain: bfloat16 [1024], P('mp'), may hold values from 0.25 to 1.75
- input_weight: bfloat16 [3, 1024, 1024], P(None, 'dp', 'mp'), may hold values from -0.125 to 0.125
- output_weight: bfloat16 [1024, 1024], P('mp', 'dp'), may hold values from -1 to 1
- position_bias: bfloat16 [16, 512, 512], P('mp'), may hold values from -3 to 353
- post_gain: bfloat16 [1024], P('mp'), may hold values from 0.25 to 1.75
Outputs:
- stream: bfloat16 [4096, 1024], P('dp', 'mp')
- normed: bfloat16 [4096, 1024], P('dp', 'mp')
All inputs are finite; a program needn't handle non-finite values.
Results may differ from a plain program's by a relative error of at most 0.013.
Values may be sent and summed in bfloat16 or wider, within the bound.
A program may use at most 64 MiB of HBM per device.

v0:
```python
import jax
import jax.numpy as jnp
from jax import lax
from jax.sharding import PartitionSpec as P

epsilon = 1e-06


def attend_all(mixed_heads, position_bias):
    row_count = mixed_heads.shape[1]
    inner_width = mixed_heads.shape[2]
    head_count = position_bias.shape[0]
    seq_len = position_bias.shape[1]
    grouped = mixed_heads.reshape(
        3, row_count // seq_len, seq_len, head_count, inner_width // head_count
    )
    bias_wide = position_bias.astype(jnp.float32)

    def one_sequence(sequence):
        sequence_block = lax.dynamic_index_in_dim(grouped, sequence, 1, keepdims=False)
        scores = (
            jnp.einsum(
                "qhd,khd->hqk",
                sequence_block[0],
                sequence_block[1],
                preferred_element_type=jnp.float32,
            )
            + bias_wide
        )
        row_max = jnp.max(scores, axis=2, keepdims=True)
        weights = jnp.exp(scores - row_max)
        probabilities = (weights / jnp.sum(weights, axis=2, keepdims=True)).astype(jnp.bfloat16)
        context = jnp.einsum(
            "hqk,khd->qhd", probabilities, sequence_block[2], preferred_element_type=jnp.float32
        )
        return context.reshape(seq_len, inner_width).astype(jnp.bfloat16)

    stacked = lax.map(one_sequence, jnp.arange(row_count // seq_len, dtype=jnp.int32))
    return stacked.reshape(row_count, inner_width)


def on_device(tokens, pre_gain, input_weight, output_weight, position_bias, post_gain):
    rows_all, gain_all = (
        lax.all_gather(tokens, "mp", axis=1, tiled=True),
        lax.all_gather(pre_gain, "mp", axis=0, tiled=True),
    )
    widened = rows_all.astype(jnp.float32)
    inverse_rms = lax.rsqrt(jnp.mean(widened * widened, axis=1, keepdims=True) + epsilon)
    normed_in = (widened * inverse_rms * gain_all.astype(jnp.float32)).astype(jnp.bfloat16)
    feature_count = tokens.shape[1]
    projected = jnp.einsum(
        "td,kdi->kti",
        normed_in,
        lax.all_gather(input_weight, "dp", axis=1, tiled=True),
        preferred_element_type=jnp.float32,
    )
    context = attend_all(projected.astype(jnp.bfloat16), position_bias)
    partial_value = jnp.dot(
        context,
        lax.all_gather(output_weight, "dp", axis=1, tiled=True),
        preferred_element_type=jnp.float32,
    )
    attention_out = lax.psum_scatter(
        partial_value.astype(jnp.bfloat16), "mp", scatter_dimension=1, tiled=True
    ).astype(jnp.float32)
    stream = (tokens.astype(jnp.float32) + attention_out).astype(jnp.bfloat16)
    restored = lax.optimization_barrier(stream).astype(jnp.float32)
    squares = lax.psum(jnp.sum(restored * restored, axis=1), "mp")
    post_rms = lax.rsqrt(squares[:, None] / (feature_count * lax.axis_size("mp")) + epsilon)
    normed = (restored * post_rms * post_gain.astype(jnp.float32)).astype(jnp.bfloat16)
    return (stream, normed)


def solution(mesh):
    return jax.shard_map(
        on_device,
        mesh=mesh,
        in_specs=(
            P("dp", "mp"),
            P("mp"),
            P(None, "dp", "mp"),
            P("mp", "dp"),
            P("mp", None, None),
            P("mp"),
        ),
        out_specs=(P("dp", "mp"), P("dp", "mp")),
        check_vma=False,
    )
```

profile of v0, /device:TPU:0, one launch (start us, length us, event | category | flops | bytes accessed | tf_op | source)
XLA Modules:
  0.0 123.4 jit_solution(2190378064825369234)
XLA Ops:
  7.2 0.0 all-gather.4.cloned.1.call-start
  7.2 0.7 all-gather.4.cloned.1.call-update
  7.9 0.0 all-gather.6.cloned.1.call-start
  7.9 1.7 %copy.11 = bf16[3,128,256]{1,2,0:T(8,128)(2,1)} copy(bf16[3,128,256]{2,1,0:T(8,128)(2,1)} %param.8) | data formatting | bytes 393216 | tf_op args[2]
  9.7 0.0 all-gather.6.cloned.1.call-update
  9.7 0.0 reduce-scatter.2.cloned.1.call-start
  9.8 0.7 reshape.34
  10.4 12.6 %all-gather = bf16[4,1,256]{2,1,0:T(2,128)(2,1)S(1)} all-gather(bf16[1,1,256]{2,1,0:T(2,128)(2,1)S(1)} %reshape.34), channel_id=1, replica_groups=mesh['dp'=8,'mp'=4] {'mp'}, dimensions={0}, use_global_device_ids=true | all-gather | bytes 2560 | tf_op jit(solution)/shard_map/all_gather | solution.py:45
  23.1 0.0 copy-start.2
  23.1 2.8 %copy.12 = bf16[4,512,512]{1,2,0:T(8,128)(2,1)S(1)} copy(bf16[4,512,512]{2,1,0:T(8,128)(2,1)} %param.10) | data formatting | bytes 4194304 | tf_op args[4]
  25.9 0.0 copy-done.2
  25.9 10.0 %all_gather.15 = bf16[256,1024]{1,0:T(8,128)(2,1)S(1)} all-gather(bf16[256,128]{1,0:T(8,128)(2,1)S(1)} %copy-done.2), channel_id=1, replica_groups=mesh['dp'=8,'mp'=4] {'dp'}, dimensions={1}, use_global_device_ids=true | all-gather | bytes 589824 | tf_op jit(solution)/shard_map/all_gather | solution.py:60
  35.9 6.2 %all-gather.4.cloned.1.call-done = bf16[512,1024]{1,0:T(8,128)(2,1)} async-done(((bf16[512,256]{1,0:T(8,128)(2,1)}), bf16[512,1024]{1,0:T(8,128)(2,1)}) %all-gather.4.cloned.1.call-update) | async-done | bytes 1048592 | tf_op jit(solution)/shard_map/all_gather | solution.py:44
  42.1 1.5 %fusion.2 = f32[512]{0:T(512)S(1)} fusion(bf16[512,1024]{1,0:T(8,128)(2,1)} %all-gather.4.cloned.1.call-done), kind=kLoop, calls=%fused_computation.7 | loop fusion | flops 1572352 | bytes 1050624 | tf_op jit(solution)/shard_map/reduce_sum | solution.py:48
  43.6 25.1 %all-gather.6.cloned.1.call-done = bf16[3,1024,256]{1,2,0:T(8,128)(2,1)} async-done(((bf16[3,128,256]{1,2,0:T(8,128)(2,1)}), bf16[3,1024,256]{1,2,0:T(8,128)(2,1)}) %all-gather.6.cloned.1.call-update) | async-done | bytes 1572880 | tf_op jit(solution)/shard_map/all_gather | solution.py:54
  68.7 2.8 %fusion.6 = bf16[3,512,256]{1,2,0:T(8,128)(2,1)S(1)} fusion(bf16[3,1024,256]{1,2,0:T(8,128)(2,1)} %all-gather.6.cloned.1.call-done, bf16[512,1024]{1,0:T(8,128)(2,1)} %all-gather.4.cloned.1.call-done, f32[1024]{0:T(1024)S(1)} %bitcast.26, f32[512]{0:T(512)S(1)} %add_rsqrt_fusion.1), kind=kOutput, calls=%fused_computation.13 | convolution fusion | flops 807796736 | bytes 3414016 | tf_op jit(solution)/shard_map/td,kdi->kti/dot_general | solution.py:51
  71.5 0.8 fusion.18
  72.3 1.5 %fusion.19 = f32[4,512]{1,0:T(4,128)S(1)} fusion(bf16[4,512,512]{1,2,0:T(8,128)(2,1)S(1)} %copy.12, bf16[512,4,64]{0,2,1:T(8,128)(2,1)S(1)} %bitcast.23, bf16[512,4,64]{0,2,1:T(8,128)(2,1)S(1)} %bitcast.21), kind=kOutput, calls=%fused_computation.29 | convolution fusion | flops 138412544 | bytes 2629632 | tf_op jit(solution)/shard_map/while/body/eval_jaxpr/sub | solution.py:31
  73.8 2.9 %fusion.7 = bf16[4,64,512]{2,1,0:T(8,128)(2,1)S(1)} fusion(bf16[512,4,64]{0,2,1:T(8,128)(2,1)} %bitcast.25, f32[4,512]{1,0:T(4,128)S(1)} %fusion.19, bf16[4,512,512]{1,2,0:T(8,128)(2,1)S(1)} %copy.12, bf16[512,4,64]{0,2,1:T(8,128)(2,1)S(1)} %bitcast.24, bf16[512,4,64]{0,2,1:T(8,128)(2,1)S(1)} %bitcast.22), kind=kOutput, calls=%fused_computation.14 | convolution fusion | flops 273811968 | bytes 3153920 | tf_op jit(solution)/shard_map/while/body/eval_jaxpr/hqk,khd->qhd/dot_general | solution.py:33
  76.6 0.0 copy-start.3
  76.6 0.0 copy-start.1
  76.6 1.4 %convolution_convert_fusion = bf16[512,1024]{1,0:T(8,128)(2,1)} fusion(bf16[512,256]{0,1:T(8,128)(2,1)S(1)} %bitcast.20, bf16[256,1024]{1,0:T(8,128)(2,1)S(1)} %all_gather.15), kind=kOutput, calls=%fused_computation.11 | convolution fusion | flops 268959744 | bytes 1835008 | tf_op jit(solution)/shard_map/dot_general | solution.py:58
  78.1 0.0 reduce-scatter.2.cloned.1.call-update
  78.1 0.0 copy-done.3
  78.1 27.4 %reduce-scatter.2.cloned.1.call-done = bf16[512,256]{1,0:T(8,128)(2,1)} async-done(((bf16[512,1024]{1,0:T(8,128)(2,1)}), bf16[512,256]{1,0:T(8,128)(2,1)}) %reduce-scatter.2.cloned.1.call-update) | async-done | bytes 262160 | tf_op jit(solution)/shard_map/reduce_scatter | solution.py:63
  105.6 0.0 copy-done.1
  105.6 1.0 add_convert_fusion
  106.6 0.0 copy-start
  106.6 0.1 fusion.12
  106.7 9.3 %psum.7 = f32[512]{0:T(512)S(1)} all-reduce(f32[512]{0:T(512)S(1)} %fusion.12), channel_id=1, replica_groups=mesh['dp'=8,'mp'=4] {'mp'}, use_global_device_ids=true, to_apply=%region_5.6 | all-reduce | flops 512 | bytes 4096 | tf_op jit(solution)/shard_map/psum | solution.py:68
  116.0 0.8 fusion.14
  116.9 0.0 copy-done
  (4 shorter events, 0.0 us)
Async XLA Ops:
  7.2 35.0 %all-gather.4.cloned.1.call-start = ((), (), s32[]{:S(2)}) async-start(), calls=%async_computation.1 | async-start | bytes 1310720 | tf_op jit(solution)/shard_map/all_gather | solution.py:44
  7.9 60.8 %all-gather.6.cloned.1.call-start = ((), (), s32[]{:S(2)}) async-start(), calls=%async_computation.2 | async-start | bytes 1769472 | tf_op jit(solution)/shard_map/all_gather | solution.py:54
  9.7 95.8 %reduce-scatter.2.cloned.1.call-start = ((), (), s32[]{:S(2)}) async-start(), calls=%async_computation.3 | async-start | bytes 1310720 | tf_op jit(solution)/shard_map/reduce_scatter | solution.py:63
  23.1 2.8 %copy-start.2 = (bf16[256,128]{1,0:T(8,128)(2,1)S(1)}, bf16[256,128]{1,0:T(8,128)(2,1)}, u32[]{:S(2)}) copy-start(bf16[256,128]{1,0:T(8,128)(2,1)} %param.9) | copy-start | bytes 196612
  76.6 1.5 %copy-start.3 = (bf16[256]{0:T(256)(128)(2,1)S(1)}, bf16[256]{0:T(256)(128)(2,1)}, u32[]{:S(2)}) copy-start(bf16[256]{0:T(256)(128)(2,1)} %param.11) | copy-start | bytes 1540
  76.6 28.9 %copy-start.1 = (bf16[512,256]{1,0:T(8,128)(2,1)S(1)}, bf16[512,256]{1,0:T(8,128)(2,1)}, u32[]{:S(2)}) copy-start(bf16[512,256]{1,0:T(8,128)(2,1)} %param.6) | copy-start | bytes 786436
  106.6 10.3 %copy-start = (bf16[512,256]{1,0:T(8,128)(2,1)}, bf16[512,256]{1,0:T(8,128)(2,1)S(1)}, u32[]{:S(2)}) copy-start(bf16[512,256]{1,0:T(8,128)(2,1)S(1)} %add_convert_fusion) | copy-start | bytes 786436
Sparse Core Ops, SparseCore 0:
  9.5 32.5 all-gather.3
  44.6 24.0 all-gather.5
  78.2 27.2 reduce-scatter.1
where the time goes:
time: 124 us; the launch traced here: 123 us
  waiting for transfers between devices  59.4 us (48%)
  blocking collectives  31.9 us (26%)
  between operations  13.8 us (11%)
  matrix products  8.6 us (7%)
  local copies, waits for them, and re-layouts  6 us (5%)
  other arithmetic  3.54 us (3%)
    reduce_scatter x1, waiting for transfers between devices, on_device(): lax.psum_scatter(partial_value.astype(jnp.bfloat16), 'mp', scatter_dimens...  27.4 us
    all_gather x1, waiting for transfers between devices, on_device(): lax.all_gather(input_weight, 'dp', axis=1, tiled=True)  25.1 us
    all_gather x1, blocking collectives, on_device(): lax.all_gather(pre_gain, 'mp', axis=0, tiled=True)  12.6 us
    all_gather x1, blocking collectives, on_device(): lax.all_gather(output_weight, 'dp', axis=1, tiled=True)  9.99 us
    psum x1, blocking collectives, on_device(): squares = lax.psum(jnp.sum(restored * restored, axis=1), 'mp')  9.28 us
    all_gather x1, waiting for transfers between devices, on_device(): lax.all_gather(tokens, 'mp', axis=1, tiled=True)  6.23 us
    unnamed x11, local copies, waits for them, and re-layouts  5.24 us
    dot_general x1, matrix products, one_sequence(): jnp.einsum('hqk,khd->qhd', probabilities, sequence_block[2], preferred_el...  2.86 us
  transfers between devices with their start and end apart: 3, of which 3 were waited for; matrix products, arithmetic and copies ran while one was open for 5% of the time, Pallas kernels for 0%

commit v1 on v0

--- a/solution.py
+++ b/solution.py
@@ -4,6 +4,22 @@
 from jax.sharding import PartitionSpec as P
 
 epsilon = 1e-06
+
+
+def ring_product(shard, axis, dim, term):
+    devices, index, rows = (lax.axis_size(axis), lax.axis_index(axis), shard.shape[dim])
+    ahead = [(i, (i + 1) % devices) for i in range(devices)]
+    left = [(i, (i - 1) % devices) for i in range(devices)]
+    halfway = devices // 2
+    from_left = from_right = shard
+    total = term(shard, index * rows)
+    for step in range(1, halfway + 1):
+        from_left = lax.ppermute(from_left, axis, ahead)
+        if step < devices - halfway:
+            from_right = lax.ppermute(from_right, axis, left)
+            total = total + term(from_right, (index + step) % devices * rows)
+        total = total + term(from_left, (index - step) % devices * rows)
+    return total
 
 
 def attend_all(mixed_heads, position_bias):
@@ -48,11 +64,16 @@
     inverse_rms = lax.rsqrt(jnp.mean(widened * widened, axis=1, keepdims=True) + epsilon)
     normed_in = (widened * inverse_rms * gain_all.astype(jnp.float32)).astype(jnp.bfloat16)
     feature_count = tokens.shape[1]
-    projected = jnp.einsum(
-        "td,kdi->kti",
-        normed_in,
-        lax.all_gather(input_weight, "dp", axis=1, tiled=True),
-        preferred_element_type=jnp.float32,
+    projected = ring_product(
+        input_weight,
+        "dp",
+        1,
+        lambda shard, start: jnp.einsum(
+            "td,kdi->kti",
+            lax.dynamic_slice_in_dim(normed_in, start, shard.shape[1], axis=1),
+            shard,
+            preferred_element_type=jnp.float32,
+        ),
     )
     context = attend_all(projected.astype(jnp.bfloat16), position_bias)
     partial_value = jnp.dot(

time: 124 us -> 114 us (0.919)
  waiting for transfers between devices: 59.4 us -> 33.1 us
  starting transfers between devices: 0.12 us -> 7.87 us
  matrix products: 8.6 us -> 12.8 us
  blocking collectives: 31.9 us -> 35 us
  other arithmetic: 3.54 us -> 5.07 us
    all_gather x1 -> x0, waiting for transfers between devices: 25.1 us -> none  [on_device(): lax.all_gather(input_weight, 'dp', axis=1, tiled=True)]
    ppermute x0 -> x7, starting transfers between devices: none -> 7.8 us  [the longest x3 7.2 us: ring_product(): from_right = lax.ppermute(from_right, axis, left)]
    ppermute x0 -> x7, waiting for transfers between devices: none -> 6.58 us  [the longest x4 5.65 us: ring_product(): from_left = lax.ppermute(from_left, axis, ahead)]
    all_gather x1, waiting for transfers between devices: 6.23 us -> 0.01 us  [on_device(): lax.all_gather(tokens, 'mp', axis=1, tiled=True)]
    dot_general x1 -> x8, matrix products: 2.82 us -> 7.06 us  [on_device(): jnp.einsum('td,kdi->kti', lax.dynamic_slice_in_dim(normed_in, start, shar...]
    all_gather x1, blocking collectives: 9.99 us -> 12.7 us  [on_device(): lax.all_gather(output_weight, 'dp', axis=1, tiled=True)]
    reduce_scatter x1, waiting for transfers between devices: 27.4 us -> 25.9 us  [on_device(): lax.psum_scatter(partial_value.astype(jnp.bfloat16), 'mp', scatter_dimens...]
    convert_element_type x0 -> x1, other arithmetic: none -> 1.53 us  [on_device(): (widened * inverse_rms * gain_all.astype(jnp.float32)).astype(jnp.bfloat16)]
  transfers between devices with their start and end apart: 3 -> 9, of which waited for: 3 -> 4; matrix products, arithmetic and copies ran while one was open for 5% -> 12% of each run, Pallas kernels for 0% -> 0%
where the time goes in v1:
time: 114 us
  blocking collectives  35 us (31%)
  waiting for transfers between devices  33.1 us (29%)
  between operations  14.3 us (13%)
  matrix products  12.8 us (11%)
  starting transfers between devices  7.87 us (7%)
  local copies, waits for them, and re-layouts  5.35 us (5%)
  other arithmetic  5.07 us (4%)
    reduce_scatter x1, waiting for transfers between devices, on_device(): lax.psum_scatter(partial_value.astype(jnp.bfloat16), 'mp', scatter_dimens...  25.9 us
    all_gather x1, blocking collectives, on_device(): lax.all_gather(pre_gain, 'mp', axis=0, tiled=True)  13 us
    all_gather x1, blocking collectives, on_device(): lax.all_gather(output_weight, 'dp', axis=1, tiled=True)  12.7 us
    psum x1, blocking collectives, on_device(): squares = lax.psum(jnp.sum(restored * restored, axis=1), 'mp')  9.26 us
    ppermute x3, starting transfers between devices, ring_product(): from_right = lax.ppermute(from_right, axis, left)  7.2 us
    dot_general x8, matrix products, on_device(): jnp.einsum('td,kdi->kti', lax.dynamic_slice_in_dim(normed_in, start, shar...  7.06 us
    ppermute x4, waiting for transfers between devices, ring_product(): from_left = lax.ppermute(from_left, axis, ahead)  5.65 us
    unnamed x13, local copies, waits for them, and re-layouts  4.6 us
  transfers between devices with their start and end apart: 9, of which 4 were waited for; matrix products, arithmetic and copies ran while one was open for 12% of the time, Pallas kernels for 0%

profile of v1, /device:TPU:0, one launch (start us, length us, event | category | flops | bytes accessed | tf_op | source)
XLA Modules:
  0.0 113.5 jit_solution(754326572784996511)
XLA Ops:
  7.2 0.7 all-gather.3.cloned.1.call-update
  7.9 1.1 copy.14
  9.0 0.5 collective-permute-start.1
  9.6 2.9 %collective-permute-start = (bf16[3,128,256]{1,2,0:T(8,128)(2,1)S(1)}, bf16[3,128,256]{1,2,0:T(8,128)(2,1)S(1)}, u32[]{:S(2)}, u32[]{:S(2)}) collective-permute-start(bf16[3,128,256]{1,2,0:T(8,128)(2,1)S(1)} %copy.14), channel_id=1, source_target_pairs={{0,28},{4,0},{8,4},{12,8},{16,12},{20,16},{24,20},{28,24},{1,29},{... | collective-permute-start | bytes 589832 | tf_op jit(solution)/shard_map/ppermute | solution.py:19
  12.5 3.3 %collective-permute-done.1 = bf16[3,128,256]{1,2,0:T(8,128)(2,1)S(1)} collective-permute-done((bf16[3,128,256]{1,2,0:T(8,128)(2,1)S(1)}, bf16[3,128,256]{1,2,0:T(8,128)(2,1)S(1)}, u32[]{:S(2)}, u32[]{:S(2)}) %collective-permute-start.1) | collective-permute-done | bytes 196640 | tf_op jit(solution)/shard_map/ppermute | solution.py:17
  15.9 0.9 collective-permute-done
  16.8 2.8 %collective-permute-start.2 = (bf16[3,128,256]{1,2,0:T(8,128)(2,1)S(1)}, bf16[3,128,256]{1,2,0:T(8,128)(2,1)S(1)}, u32[]{:S(2)}, u32[]{:S(2)}) collective-permute-start(bf16[3,128,256]{1,2,0:T(8,128)(2,1)S(1)} %collective-permute-done), channel_id=1, source_target_pairs={{0,28},{4,0},{8,4},{12,8},{16,12},{20,16},{24,20},{28,24},{1,29},{... | collective-permute-start | bytes 589832 | tf_op jit(solution)/shard_map/ppermute | solution.py:19
  19.6 2.4 %collective-permute-done.3 = bf16[3,128,256]{1,2,0:T(8,128)(2,1)} collective-permute-done((bf16[3,128,256]{1,2,0:T(8,128)(2,1)S(1)}, bf16[3,128,256]{1,2,0:T(8,128)(2,1)}, u32[]{:S(2)}, u32[]{:S(2)}) %collective-permute-start.3) | collective-permute-done | bytes 196640 | tf_op jit(solution)/shard_map/ppermute | solution.py:17
  21.9 0.7 reshape.34
  22.6 13.0 %all-gather = bf16[4,1,256]{2,1,0:T(2,128)(2,1)S(1)} all-gather(bf16[1,1,256]{2,1,0:T(2,128)(2,1)S(1)} %reshape.34), channel_id=1, replica_groups=mesh['dp'=8,'mp'=4] {'mp'}, dimensions={0}, use_global_device_ids=true | all-gather | bytes 2560 | tf_op jit(solution)/shard_map/all_gather | solution.py:61
  35.6 2.8 %copy.16 = bf16[4,512,512]{1,2,0:T(8,128)(2,1)S(1)} copy(bf16[4,512,512]{2,1,0:T(8,128)(2,1)} %param.10) | data formatting | bytes 4194304 | tf_op args[4]
  38.5 12.7 %all_gather.11 = bf16[256,1024]{1,0:T(8,128)(2,1)S(1)} all-gather(bf16[256,128]{1,0:T(8,128)(2,1)S(1)} %copy-done.3), channel_id=1, replica_groups=mesh['dp'=8,'mp'=4] {'dp'}, dimensions={1}, use_global_device_ids=true | all-gather | bytes 589824 | tf_op jit(solution)/shard_map/all_gather | solution.py:81
  51.2 1.5 %collective-permute-start.4 = (bf16[3,128,256]{1,2,0:T(8,128)(2,1)S(1)}, bf16[3,128,256]{1,2,0:T(8,128)(2,1)}, u32[]{:S(2)}, u32[]{:S(2)}) collective-permute-start(bf16[3,128,256]{1,2,0:T(8,128)(2,1)S(1)} %collective-permute-done.2), channel_id=1, source_target_pairs={{0,28},{4,0},{8,4},{12,8},{16,12},{20,16},{24,20},{28,24},{1,29},{... | collective-permute-start | bytes 589832 | tf_op jit(solution)/shard_map/ppermute | solution.py:19
  52.7 1.5 %fusion.2 = f32[512]{0:T(512)S(1)} fusion(bf16[512,1024]{1,0:T(8,128)(2,1)} %all-gather.3.cloned.1.call-done), kind=kLoop, calls=%fused_computation.7 | loop fusion | flops 1572352 | bytes 1050624 | tf_op jit(solution)/shard_map/reduce_sum | solution.py:64
  54.2 1.5 %fusion.4 = bf16[512,1024]{1,0:T(8,128)(2,1)S(1)} fusion(bf16[512,1024]{1,0:T(8,128)(2,1)} %all-gather.3.cloned.1.call-done, f32[1024]{0:T(1024)S(1)} %bitcast.54, f32[512]{0:T(512)S(1)} %add_rsqrt_fusion.1), kind=kLoop, calls=%fused_computation.9 | loop fusion | flops 2097152 | bytes 2103296 | tf_op jit(solution)/shard_map/convert_element_type | solution.py:65
  55.8 0.4 fusion.26
  56.2 1.3 %fusion.14 = f32[512,3,256]{0,2,1:T(8,128)S(1)} fusion(bf16[3,128,256]{1,2,0:T(8,128)(2,1)} %collective-permute-done.5, bf16[512,1024]{1,0:T(8,128)(2,1)S(1)} %fusion.4, s32[]{:T(128)S(6)} %select_n.70), kind=kOutput, calls=%fused_computation.23 | convolution fusion | flops 100663296 | bytes 1900548 | tf_op jit(solution)/shard_map/td,kdi->kti/dot_general | solution.py:71
  57.5 1.3 %fusion.18 = f32[512,3,256]{0,2,1:T(8,128)S(1)} fusion(bf16[3,128,256]{1,2,0:T(8,128)(2,1)} %collective-permute-done.3, bf16[512,1024]{1,0:T(8,128)(2,1)S(1)} %fusion.4, s32[]{:T(128)S(6)} %select_n.66), kind=kOutput, calls=%fused_computation.27 | convolution fusion | flops 100663296 | bytes 1900548 | tf_op jit(solution)/shard_map/td,kdi->kti/dot_general | solution.py:71
  58.8 0.4 fusion.20
  59.2 0.4 fusion.22
  59.6 0.4 fusion.24
  60.0 1.3 %fusion.16 = f32[512,3,256]{0,2,1:T(8,128)S(1)} fusion(bf16[3,128,256]{1,2,0:T(8,128)(2,1)} %collective-permute-done.4, bf16[512,1024]{1,0:T(8,128)(2,1)S(1)} %fusion.4, s32[]{:T(128)S(6)} %select_n.68), kind=kOutput, calls=%fused_computation.25 | convolution fusion | flops 100663296 | bytes 1900548 | tf_op jit(solution)/shard_map/td,kdi->kti/dot_general | solution.py:71
  61.3 1.6 %fusion.6 = bf16[3,512,256]{1,2,0:T(8,128)(2,1)S(1)} fusion(bf16[3,128,256]{1,2,0:T(8,128)(2,1)} %collective-permute-done.6, f32[512,3,256]{0,2,1:T(8,128)S(1)} %fusion.14, f32[512,3,256]{0,2,1:T(8,128)S(1)} %fusion.16, f32[512,3,256]{0,2,1:T(8,128)S(1)} %fusion.18, f32[512,3,256]{0,2,1:T(8,128)S(1)} %fusion.20, f32[512,3,256]{0,2,1:T(8,128)S(1)} %fusion.22, ...), kind=kOutput, calls=%fused_computation.13 | convolution fusion | flops 103809024 | bytes 12124164 | tf_op jit(solution)/shard_map/td,kdi->kti/dot_general | solution.py:71
  62.9 0.8 fusion.45
  63.7 1.5 %fusion.46 = f32[4,512]{1,0:T(4,128)S(1)} fusion(bf16[4,512,512]{1,2,0:T(8,128)(2,1)S(1)} %copy.16, bf16[512,4,64]{0,2,1:T(8,128)(2,1)S(1)} %bitcast.51, bf16[512,4,64]{0,2,1:T(8,128)(2,1)S(1)} %bitcast.49), kind=kOutput, calls=%fused_computation.57 | convolution fusion | flops 138412544 | bytes 2629632 | tf_op jit(solution)/shard_map/while/body/eval_jaxpr/sub | solution.py:47
  65.1 2.9 %fusion.7 = bf16[4,64,512]{2,1,0:T(8,128)(2,1)S(1)} fusion(bf16[512,4,64]{0,2,1:T(8,128)(2,1)} %bitcast.53, f32[4,512]{1,0:T(4,128)S(1)} %fusion.46, bf16[4,512,512]{1,2,0:T(8,128)(2,1)S(1)} %copy.16, bf16[512,4,64]{0,2,1:T(8,128)(2,1)S(1)} %bitcast.52, bf16[512,4,64]{0,2,1:T(8,128)(2,1)S(1)} %bitcast.50), kind=kOutput, calls=%fused_computation.14 | convolution fusion | flops 273811968 | bytes 3153920 | tf_op jit(solution)/shard_map/while/body/eval_jaxpr/hqk,khd->qhd/dot_general | solution.py:49
  68.0 1.4 %convolution_convert_fusion = bf16[512,1024]{1,0:T(8,128)(2,1)} fusion(bf16[512,256]{0,1:T(8,128)(2,1)S(1)} %bitcast.48, bf16[256,1024]{1,0:T(8,128)(2,1)S(1)} %all_gather.11), kind=kOutput, calls=%fused_computation.12 | convolution fusion | flops 268959744 | bytes 1835008 | tf_op jit(solution)/shard_map/dot_general | solution.py:79
  69.5 25.9 %reduce-scatter.2.cloned.1.call-done = bf16[512,256]{1,0:T(8,128)(2,1)} async-done(((bf16[512,1024]{1,0:T(8,128)(2,1)}), bf16[512,256]{1,0:T(8,128)(2,1)}) %reduce-scatter.2.cloned.1.call-update) | async-done | bytes 262160 | tf_op jit(solution)/shard_map/reduce_scatter | solution.py:84
  95.4 1.0 add_convert_fusion.1
  96.4 0.1 fusion.8
  96.6 9.3 %psum.7 = f32[512]{0:T(512)S(1)} all-reduce(f32[512]{0:T(512)S(1)} %fusion.8), channel_id=1, replica_groups=mesh['dp'=8,'mp'=4] {'mp'}, use_global_device_ids=true, to_apply=%region_5.6 | all-reduce | flops 512 | bytes 4096 | tf_op jit(solution)/shard_map/psum | solution.py:89
  105.8 0.8 fusion.10
  (25 shorter events, 0.2 us)
Async XLA Ops:
  7.2 45.5 %all-gather.3.cloned.1.call-start = ((), (), s32[]{:S(2)}) async-start(), calls=%async_computation.1 | async-start | bytes 1310720 | tf_op jit(solution)/shard_map/all_gather | solution.py:60
  7.9 87.5 %reduce-scatter.2.cloned.1.call-start = ((), (), s32[]{:S(2)}) async-start(), calls=%async_computation.2 | async-start | bytes 1310720 | tf_op jit(solution)/shard_map/reduce_scatter | solution.py:84
  9.0 6.8 %collective-permute-start.1 = (bf16[3,128,256]{1,2,0:T(8,128)(2,1)S(1)}, bf16[3,128,256]{1,2,0:T(8,128)(2,1)S(1)}, u32[]{:S(2)}, u32[]{:S(2)}) collective-permute-start(bf16[3,128,256]{1,2,0:T(8,128)(2,1)S(1)} %copy.14), channel_id=1, source_target_pairs={{0,4},{4,8},{8,12},{12,16},{16,20},{20,24},{24,28},{28,0},{1,5},{5... | collective-permute-start | bytes 589832 | tf_op jit(solution)/shard_map/ppermute | solution.py:17
  9.6 7.2 %collective-permute-start = (bf16[3,128,256]{1,2,0:T(8,128)(2,1)S(1)}, bf16[3,128,256]{1,2,0:T(8,128)(2,1)S(1)}, u32[]{:S(2)}, u32[]{:S(2)}) collective-permute-start(bf16[3,128,256]{1,2,0:T(8,128)(2,1)S(1)} %copy.14), channel_id=1, source_target_pairs={{0,28},{4,0},{8,4},{12,8},{16,12},{20,16},{24,20},{28,24},{1,29},{... | collective-permute-start | bytes 589832 | tf_op jit(solution)/shard_map/ppermute | solution.py:19
  15.8 6.1 %collective-permute-start.3 = (bf16[3,128,256]{1,2,0:T(8,128)(2,1)S(1)}, bf16[3,128,256]{1,2,0:T(8,128)(2,1)}, u32[]{:S(2)}, u32[]{:S(2)}) collective-permute-start(bf16[3,128,256]{1,2,0:T(8,128)(2,1)S(1)} %collective-permute-done.1), channel_id=1, source_target_pairs={{0,4},{4,8},{8,12},{12,16},{16,20},{20,24},{24,28},{28,0},{1,5},{5... | collective-permute-start | bytes 589832 | tf_op jit(solution)/shard_map/ppermute | solution.py:17
  16.8 34.5 %collective-permute-start.2 = (bf16[3,128,256]{1,2,0:T(8,128)(2,1)S(1)}, bf16[3,128,256]{1,2,0:T(8,128)(2,1)S(1)}, u32[]{:S(2)}, u32[]{:S(2)}) collective-permute-start(bf16[3,128,256]{1,2,0:T(8,128)(2,1)S(1)} %collective-permute-done), channel_id=1, source_target_pairs={{0,28},{4,0},{8,4},{12,8},{16,12},{20,16},{24,20},{28,24},{1,29},{... | collective-permute-start | bytes 589832 | tf_op jit(solution)/shard_map/ppermute | solution.py:19
  21.9 30.8 %collective-permute-start.5 = (bf16[3,128,256]{1,2,0:T(8,128)(2,1)}, bf16[3,128,256]{1,2,0:T(8,128)(2,1)}, u32[]{:S(2)}, u32[]{:S(2)}) collective-permute-start(bf16[3,128,256]{1,2,0:T(8,128)(2,1)} %collective-permute-done.3), channel_id=1, source_target_pairs={{0,4},{4,8},{8,12},{12,16},{16,20},{20,24},{24,28},{28,0},{1,5},{5... | collective-permute-start | bytes 589832 | tf_op jit(solution)/shard_map/ppermute | solution.py:17
  35.6 2.9 %copy-start.3 = (bf16[256,128]{1,0:T(8,128)(2,1)S(1)}, bf16[256,128]{1,0:T(8,128)(2,1)}, u32[]{:S(2)}) copy-start(bf16[256,128]{1,0:T(8,128)(2,1)} %param.9) | copy-start | bytes 196612
  38.5 17.3 %copy-start.2 = (bf16[3,128,256]{2,1,0:T(8,128)(2,1)S(1)}, bf16[3,128,256]{2,1,0:T(8,128)(2,1)}, u32[]{:S(2)}) copy-start(bf16[3,128,256]{2,1,0:T(8,128)(2,1)} %param.8) | copy-start | bytes 589828
  51.2 8.7 %collective-permute-start.4 = (bf16[3,128,256]{1,2,0:T(8,128)(2,1)S(1)}, bf16[3,128,256]{1,2,0:T(8,128)(2,1)}, u32[]{:S(2)}, u32[]{:S(2)}) collective-permute-start(bf16[3,128,256]{1,2,0:T(8,128)(2,1)S(1)} %collective-permute-done.2), channel_id=1, source_target_pairs={{0,28},{4,0},{8,4},{12,8},{16,12},{20,16},{24,20},{28,24},{1,29},{... | collective-permute-start | bytes 589832 | tf_op jit(solution)/shard_map/ppermute | solution.py:19
  52.7 8.6 %collective-permute-start.6 = (bf16[3,128,256]{1,2,0:T(8,128)(2,1)}, bf16[3,128,256]{1,2,0:T(8,128)(2,1)}, u32[]{:S(2)}, u32[]{:S(2)}) collective-permute-start(bf16[3,128,256]{1,2,0:T(8,128)(2,1)} %collective-permute-done.5), channel_id=1, source_target_pairs={{0,4},{4,8},{8,12},{12,16},{16,20},{20,24},{24,28},{28,0},{1,5},{5... | collective-permute-start | bytes 589832 | tf_op jit(solution)/shard_map/ppermute | solution.py:17
  68.0 1.5 %copy-start.4 = (bf16[256]{0:T(256)(128)(2,1)S(1)}, bf16[256]{0:T(256)(128)(2,1)}, u32[]{:S(2)}) copy-start(bf16[256]{0:T(256)(128)(2,1)} %param.11) | copy-start | bytes 1540
  68.0 27.4 %copy-start.1 = (bf16[512,256]{1,0:T(8,128)(2,1)S(1)}, bf16[512,256]{1,0:T(8,128)(2,1)}, u32[]{:S(2)}) copy-start(bf16[512,256]{1,0:T(8,128)(2,1)} %param.6) | copy-start | bytes 786436
  96.4 10.3 %copy-start = (bf16[512,256]{1,0:T(8,128)(2,1)}, bf16[512,256]{1,0:T(8,128)(2,1)S(1)}, u32[]{:S(2)}) copy-start(bf16[512,256]{1,0:T(8,128)(2,1)S(1)} %add_convert_fusion.1) | copy-start | bytes 786436
Sparse Core Ops, SparseCore 0:
  9.5 32.7 all-gather.2
  69.6 25.7 reduce-scatter.1
